TPU v7x, 32 devices: a whole 2x2x4 slice. The times are simulated.
32 devices in a mesh: ov: 16 (over z, y, core), vec: 2 (over x).
Axes of the slice: x: 2, y: 2, z: 4, core: 2. Of those that a mesh axis runs over, the one named last changes fastest.
Arguments:
- chol_vectors: bfloat16 [196608, 4096], P('ov', 'vec'), may hold values from -3.5 to 3.5
- amplitudes: bfloat16 [196608, 256], P('ov'), may hold values from -0.013671875 to 0.013671875
- sigma_prior: bfloat16 [196608, 256], P(('ov', 'vec')), may hold values from -4 to 4
Outputs:
- sigma_cycle: bfloat16 [196608, 256], P(('ov', 'vec'))
All inputs are finite; a program needn't handle non-finite values.
Results may differ from a plain program's by a relative error of at most 0.0065.
Values may be sent and summed in bfloat16 or wider, within the bound.
A program may use at most 128 MiB of HBM per device.

v0:
```python
import jax
import jax.numpy as jnp
from jax import lax
from jax.sharding import PartitionSpec as P


def body(chol_vectors, amplitudes, sigma_prior):
    contract = (((0,), (0,)), ((), ()))
    partial_x = lax.dot_general(
        chol_vectors, amplitudes, contract, preferred_element_type=jnp.float32
    )
    summed = lax.psum(partial_x, "ov")
    coupling = summed.astype(jnp.bfloat16)
    cycle = lax.psum_scatter(
        jnp.dot(chol_vectors, coupling, preferred_element_type=jnp.float32),
        "vec",
        scatter_dimension=0,
        tiled=True,
    )
    return (sigma_prior.astype(jnp.float32) + cycle).astype(jnp.bfloat16)


def solution(mesh):
    return jax.shard_map(
        body,
        mesh=mesh,
        in_specs=(P("ov", "vec"), P("ov", None), P(("ov", "vec"), None)),
        out_specs=P(("ov", "vec"), None),
        check_vma=False,
    )
```

profile of v0, /device:TPU:0, one launch (start us, length us, event | category | flops | bytes accessed | tf_op | source)
XLA Modules:
  0.0 287.8 jit_solution(18080904443797007626)
XLA Ops:
  6.5 0.0 reduce-scatter.2.cloned.1.call-start
  6.5 21.7 %fusion.1 = f32[2048,256]{1,0:T(8,128)S(1)} fusion(bf16[12288,2048]{1,0:T(8,128)(2,1)} %param.3, bf16[12288,256]{1,0:T(8,128)(2,1)} %param.4), kind=kOutput, calls=%fused_computation.3 | convolution fusion | flops 12884901888 | bytes 58720256 | tf_op jit(solution)/shard_map/dot_general | solution.py:9
  28.3 76.9 %all-reduce.1 = bf16[2048,256]{1,0:T(8,128)(2,1)S(1)} all-reduce(f32[2048,256]{1,0:T(8,128)S(1)} %fusion.1), channel_id=1, replica_groups=mesh['ov'=16,'vec'=2] {'ov'}, use_global_device_ids=true, to_apply=%region_0.0 | all-reduce | flops 524288 | bytes 3145728 | tf_op jit(solution)/shard_map/psum | solution.py:12
  105.1 23.9 %convolution_bitcast_fusion = f32[12288,256]{0,1:T(8,128)} fusion(bf16[12288,2048]{1,0:T(8,128)(2,1)} %param.3, bf16[2048,256]{1,0:T(8,128)(2,1)S(1)} %all-reduce.1), kind=kOutput, calls=%fused_computation | convolution fusion | flops 12884901888 | bytes 63963136 | tf_op jit(solution)/shard_map/dot_general | solution.py:15
  129.1 0.0 reduce-scatter.2.cloned.1.call-update
  129.1 3.2 %copy.4 = bf16[6144,256]{0,1:T(8,128)(2,1)S(1)} copy(bf16[6144,256]{1,0:T(8,128)(2,1)} %param.5) | data formatting | bytes 6291456 | tf_op args[2]
  132.3 138.7 %reduce-scatter.2.cloned.1.call-done = f32[6144,256]{0,1:T(8,128)} async-done(((f32[12288,256]{0,1:T(8,128)}), f32[6144,256]{0,1:T(8,128)}) %reduce-scatter.2.cloned.1.call-update) | async-done | bytes 6291472 | tf_op jit(solution)/shard_map/reduce_scatter | solution.py:14
  271.0 5.3 %add_convert_fusion = bf16[6144,256]{0,1:T(8,128)(2,1)} fusion(f32[6144,256]{0,1:T(8,128)} %reduce-scatter.2.cloned.1.call-done, bf16[6144,256]{0,1:T(8,128)(2,1)S(1)} %copy.4), kind=kLoop, calls=%fused_computation.1 | loop fusion | flops 4718592 | bytes 12582912 | tf_op jit(solution)/shard_map/convert_element_type | solution.py:20
  276.3 4.6 %copy.5 = bf16[6144,256]{1,0:T(8,128)(2,1)} copy(bf16[6144,256]{0,1:T(8,128)(2,1)} %add_convert_fusion) | data formatting | bytes 6291456 | tf_op jit(solution)/shard_map/convert_element_type | solution.py:20
Async XLA Ops:
  6.5 264.5 %reduce-scatter.2.cloned.1.call-start = ((), (), s32[]{:S(2)}) async-start(), calls=%async_computation.1 | async-start | bytes 18874368 | tf_op jit(solution)/shard_map/reduce_scatter | solution.py:14
Sparse Core Ops, SparseCore 0:
  129.2 141.7 reduce-scatter.1
where the time goes:
time: 288 us
  waiting for transfers between devices  139 us (48%)
  blocking collectives  76.9 us (27%)
  matrix products  45.6 us (16%)
  between operations  13.4 us (5%)
  local copies, waits for them, and re-layouts  7.82 us (3%)
  other arithmetic  5.28 us (2%)
    reduce_scatter x1, waiting for transfers between devices, body(): lax.psum_scatter(jnp.dot(chol_vectors, coupling, preferred_element_type=j...  139 us
    psum x1, blocking collectives, body(): summed = lax.psum(partial_x, 'ov')  76.9 us
    dot_general x1, matrix products, body(): jnp.dot(chol_vectors, coupling, preferred_element_type=jnp.float32)  23.9 us
    dot_general x1, matrix products, body(): lax.dot_general(chol_vectors, amplitudes, contract, preferred_element_typ...  21.7 us
  transfers between devices with their start and end apart: 1, of which 1 were waited for; matrix products, arithmetic and copies ran while one was open for 1% of the time, Pallas kernels for 0%

commit v1 on v0

--- a/solution.py
+++ b/solution.py
@@ -9,7 +9,10 @@
     partial_x = lax.dot_general(
         chol_vectors, amplitudes, contract, preferred_element_type=jnp.float32
     )
-    summed = lax.psum(partial_x, "ov")
+    size, summed = (lax.axis_size("ov"), partial_x)
+    for stride in [1 << k for k in range(size.bit_length() - 1)]:
+        swap = [(i, i ^ stride) for i in range(size)]
+        summed = summed + lax.ppermute(summed, "ov", swap)
     coupling = summed.astype(jnp.bfloat16)
     cycle = lax.psum_scatter(
         jnp.dot(chol_vectors, coupling, preferred_element_type=jnp.float32),

time: 288 us -> 409 us (1.42)
  waiting for transfers between devices: 139 us -> 327 us
  blocking collectives: 76.9 us -> 0 us
  starting transfers between devices: 0.01 us -> 7.96 us
    ppermute x0 -> x4, waiting for transfers between devices: none -> 185 us  [body(): summed = summed + lax.ppermute(summed, 'ov', swap)]
    psum x1 -> x0, blocking collectives: 76.9 us -> none  [body(): summed = lax.psum(partial_x, 'ov')]
    ppermute x0 -> x4, starting transfers between devices: none -> 7.96 us  [body(): summed = summed + lax.ppermute(summed, 'ov', swap)]
  transfers between devices with their start and end apart: 1 -> 5, of which waited for: 1 -> 5; matrix products, arithmetic and copies ran while one was open for 1% -> 1% of each run, Pallas kernels for 0% -> 0%
where the time goes in v1:
time: 409 us; the launch traced here: 408 us
  waiting for transfers between devices  327 us (80%)
  matrix products  46.2 us (11%)
  between operations  13.4 us (3%)
  starting transfers between devices  7.96 us (2%)
  local copies, waits for them, and re-layouts  7.82 us (2%)
  other arithmetic  6.07 us (1%)
    ppermute x4, waiting for transfers between devices, body(): summed = summed + lax.ppermute(summed, 'ov', swap)  185 us
    reduce_scatter x1, waiting for transfers between devices, body(): lax.psum_scatter(jnp.dot(chol_vectors, coupling, preferred_element_type=j...  142 us
    dot_general x1, matrix products, body(): jnp.dot(chol_vectors, coupling, preferred_element_type=jnp.float32)  24.5 us
    dot_general x1, matrix products, body(): lax.dot_general(chol_vectors, amplitudes, contract, preferred_element_typ...  21.7 us
  transfers between devices with their start and end apart: 5, of which 5 were waited for; matrix products, arithmetic and copies ran while one was open for 1% of the time, Pallas kernels for 0%

profile of v1, /device:TPU:0, one launch (start us, length us, event | category | flops | bytes accessed | tf_op | source)
XLA Modules:
  0.0 408.4 jit_solution(15865993328646608873)
XLA Ops:
  6.5 0.0 reduce-scatter.2.cloned.1.call-start
  6.5 21.7 %fusion = f32[2048,256]{1,0:T(8,128)S(1)} fusion(bf16[12288,2048]{1,0:T(8,128)(2,1)} %param.3, bf16[12288,256]{1,0:T(8,128)(2,1)} %param.4), kind=kOutput, calls=%fused_computation.3 | convolution fusion | flops 12884901888 | bytes 58720256 | tf_op jit(solution)/shard_map/dot_general | solution.py:9
  28.3 0.6 collective-permute-start
  28.8 3.8 collective-permute-done
  32.6 0.3 add.17
  32.9 2.9 collective-permute-start.1
  35.8 45.9 %collective-permute-done.1 = f32[2048,256]{1,0:T(8,128)S(1)} collective-permute-done((f32[2048,256]{1,0:T(8,128)S(1)}, f32[2048,256]{1,0:T(8,128)S(1)}, u32[]{:S(2)}, u32[]{:S(2)}) %collective-permute-start.1) | collective-permute-done | bytes 2097184 | tf_op jit(solution)/shard_map/ppermute | solution.py:15
  81.7 0.3 add.18
  82.0 1.9 collective-permute-start.2
  83.9 45.3 %collective-permute-done.2 = f32[2048,256]{1,0:T(8,128)S(1)} collective-permute-done((f32[2048,256]{1,0:T(8,128)S(1)}, f32[2048,256]{1,0:T(8,128)S(1)}, u32[]{:S(2)}, u32[]{:S(2)}) %collective-permute-start.2) | collective-permute-done | bytes 2097184 | tf_op jit(solution)/shard_map/ppermute | solution.py:15
  129.2 0.3 add.19
  129.4 2.6 collective-permute-start.3
  132.0 89.7 %collective-permute-done.3 = f32[2048,256]{1,0:T(8,128)} collective-permute-done((f32[2048,256]{1,0:T(8,128)S(1)}, f32[2048,256]{1,0:T(8,128)}, u32[]{:S(2)}, u32[]{:S(2)}) %collective-permute-start.3) | collective-permute-done | bytes 2097184 | tf_op jit(solution)/shard_map/ppermute | solution.py:15
  221.7 24.5 %convolution_bitcast_fusion = f32[12288,256]{0,1:T(8,128)} fusion(bf16[12288,2048]{1,0:T(8,128)(2,1)} %param.3, f32[2048,256]{1,0:T(8,128)S(1)} %add.19, f32[2048,256]{1,0:T(8,128)} %collective-permute-done.3), kind=kOutput, calls=%fused_computation | convolution fusion | flops 12885950464 | bytes 67108864 | tf_op jit(solution)/shard_map/dot_general | solution.py:18
  246.2 0.0 reduce-scatter.2.cloned.1.call-update
  246.2 3.2 copy.4
  249.4 142.3 %reduce-scatter.2.cloned.1.call-done = f32[6144,256]{0,1:T(8,128)} async-done(((f32[12288,256]{0,1:T(8,128)}), f32[6144,256]{0,1:T(8,128)}) %reduce-scatter.2.cloned.1.call-update) | async-done | bytes 6291472 | tf_op jit(solution)/shard_map/reduce_scatter | solution.py:17
  391.7 5.3 %add_convert_fusion = bf16[6144,256]{0,1:T(8,128)(2,1)} fusion(f32[6144,256]{0,1:T(8,128)} %reduce-scatter.2.cloned.1.call-done, bf16[6144,256]{0,1:T(8,128)(2,1)S(1)} %copy.4), kind=kLoop, calls=%fused_computation.1 | loop fusion | flops 4718592 | bytes 12582912 | tf_op jit(solution)/shard_map/convert_element_type | solution.py:23
  397.0 4.6 %copy.5 = bf16[6144,256]{1,0:T(8,128)(2,1)} copy(bf16[6144,256]{0,1:T(8,128)(2,1)} %add_convert_fusion) | data formatting | bytes 6291456 | tf_op jit(solution)/shard_map/convert_element_type | solution.py:23
Async XLA Ops:
  6.5 385.2 %reduce-scatter.2.cloned.1.call-start = ((), (), s32[]{:S(2)}) async-start(), calls=%async_computation.1 | async-start | bytes 18874368 | tf_op jit(solution)/shard_map/reduce_scatter | solution.py:17
  28.3 4.3 %collective-permute-start = (f32[2048,256]{1,0:T(8,128)S(1)}, f32[2048,256]{1,0:T(8,128)S(1)}, u32[]{:S(2)}, u32[]{:S(2)}) collective-permute-start(f32[2048,256]{1,0:T(8,128)S(1)} %fusion), channel_id=1, source_target_pairs={{0,2},{2,0},{4,6},{6,4},{8,10},{10,8},{12,14},{14,12},{16,18},{18,... | collective-permute-start | bytes 6291464 | tf_op jit(solution)/shard_map/ppermute | solution.py:15
  32.9 48.9 %collective-permute-start.1 = (f32[2048,256]{1,0:T(8,128)S(1)}, f32[2048,256]{1,0:T(8,128)S(1)}, u32[]{:S(2)}, u32[]{:S(2)}) collective-permute-start(f32[2048,256]{1,0:T(8,128)S(1)} %add.17), channel_id=1, source_target_pairs={{0,4},{2,6},{4,0},{6,2},{8,12},{10,14},{12,8},{14,10},{16,20},{18,... | collective-permute-start | bytes 6291464 | tf_op jit(solution)/shard_map/ppermute | solution.py:15
  82.0 47.2 %collective-permute-start.2 = (f32[2048,256]{1,0:T(8,128)S(1)}, f32[2048,256]{1,0:T(8,128)S(1)}, u32[]{:S(2)}, u32[]{:S(2)}) collective-permute-start(f32[2048,256]{1,0:T(8,128)S(1)} %add.18), channel_id=1, source_target_pairs={{0,8},{2,10},{4,12},{6,14},{8,0},{10,2},{12,4},{14,6},{16,24},{18,... | collective-permute-start | bytes 6291464 | tf_op jit(solution)/shard_map/ppermute | solution.py:15
  129.4 92.3 %collective-permute-start.3 = (f32[2048,256]{1,0:T(8,128)S(1)}, f32[2048,256]{1,0:T(8,128)}, u32[]{:S(2)}, u32[]{:S(2)}) collective-permute-start(f32[2048,256]{1,0:T(8,128)S(1)} %add.19), channel_id=1, source_target_pairs={{0,16},{2,18},{4,20},{6,22},{8,24},{10,26},{12,28},{14,30},{16,0},... | collective-permute-start | bytes 6291464 | tf_op jit(solution)/shard_map/ppermute | solution.py:15
Sparse Core Ops, SparseCore 0:
  246.3 145.3 reduce-scatter.1
